TPU v7x, 32 devices: a whole 2x2x4 slice. The times are simulated.
32 devices in a mesh: dp: 8 (over z, x), mp: 4 (over y, core).
Axes of the slice: x: 2, y: 2, z: 4, core: 2. Of those that a mesh axis runs over, the one named last changes fastest.
Arguments:
- teacher_states: bfloat16 [512, 128, 4096], P('dp', None, 'mp'), may hold values from -6 to 6
- teacher_gain: float32 [4096], P('mp'), may hold values from 0.25 to 1.75
- teacher_proj: bfloat16 [4096, 1024], P('mp'), may hold values from -0.09375 to 0.09375
- teacher_mask: int32 [512, 128], P('dp'), may hold values 0 or 1
- student_states: bfloat16 [1024, 64, 768], P(('dp', 'mp')), may hold values from -6 to 6
- student_gain: float32 [768], replicated, may hold values from 0.25 to 1.75
- student_proj: bfloat16 [768, 1024], replicated, may hold values from -0.21875 to 0.21875
- student_mask: int32 [1024, 64], P(('dp', 'mp')), may hold values 0 or 1
- positive: int32 [1024], P(('dp', 'mp')), may hold values from 0 to 511
Outputs:
- grad_embed: float32 [1024, 1024], P(('dp', 'mp'))
- grad_states: bfloat16 [1024, 64, 768], P(('dp', 'mp'))
All inputs are finite; a program needn't handle non-finite values. No bound on the sum of `teacher_mask` or of `student_mask` on one device may be relied on, other than what follows from the above.
Results may differ from a plain program's by a relative error of at most 0.0085.
Values may be sent and summed in bfloat16 or wider, within the bound.
A program may use at most 128 MiB of HBM per device.

v0:
```python
import jax
import jax.numpy as jnp
from jax import lax
from jax.sharding import PartitionSpec as P

D = 4096


def unit_rows(values):
    return (
        values
        * lax.rsqrt(jnp.mean(values * values, axis=-1, keepdims=True) + 1e-06)
        / jnp.sqrt(jnp.float32(values.shape[-1]))
    )


def student_forward(states, gain, proj, live_mask):
    values = states.astype(jnp.float32)
    scale = lax.rsqrt(jnp.mean(values * values, axis=-1, keepdims=True) + 1e-06)
    normed = (values * scale * gain).astype(jnp.bfloat16)
    flat = normed.reshape(-1, normed.shape[-1])
    act = jax.nn.gelu(jnp.dot(flat, proj, preferred_element_type=jnp.float32), approximate=True)
    act = act.reshape(states.shape[0], states.shape[1], -1)
    live = live_mask.astype(jnp.float32)
    pooled = jnp.sum(act * live[:, :, None], axis=1)
    return unit_rows(pooled)


def shards(
    teacher_states,
    teacher_gain,
    teacher_proj,
    teacher_mask,
    student_states,
    student_gain,
    student_proj,
    student_mask,
    positive,
):
    values = teacher_states.astype(jnp.float32)
    partial_squares = jnp.sum(values * values, axis=-1)
    squares = lax.psum(partial_squares, "mp")
    scale = lax.rsqrt(squares / D + 1e-06)
    live = teacher_mask.astype(jnp.float32)
    weight = live * scale
    pooled = jnp.sum(values * weight[:, :, None], axis=1)
    tpooled = (pooled * teacher_gain).astype(jnp.bfloat16)
    partial_embed = jnp.dot(tpooled, teacher_proj, preferred_element_type=jnp.float32)
    summed = lax.psum(partial_embed, "mp")
    group_emb = unit_rows(summed).astype(jnp.bfloat16)
    gathered = lax.all_gather(group_emb, "dp", axis=0, tiled=True)
    semb, back = jax.vjp(
        lambda st: student_forward(st, student_gain, student_proj, student_mask), student_states
    )
    sround = semb.astype(jnp.bfloat16)
    columns = lax.broadcasted_iota(jnp.int32, (positive.shape[0], gathered.shape[0]), 1)
    picker = (positive[:, None] == columns).astype(jnp.bfloat16)
    tpos = jnp.dot(picker, gathered, preferred_element_type=jnp.float32).astype(jnp.bfloat16)
    tlogit = 10.0 * jnp.dot(tpos, gathered.T, preferred_element_type=jnp.float32)
    slogit = 20.0 * jnp.dot(sround, gathered.T, preferred_element_type=jnp.float32)
    texp = jnp.exp(tlogit)
    sexp = jnp.exp(slogit)
    diff = (
        sexp / jnp.sum(sexp, axis=1, keepdims=True) - texp / jnp.sum(texp, axis=1, keepdims=True)
    ).astype(jnp.bfloat16)
    grad_embed = 20.0 * jnp.dot(diff, gathered, preferred_element_type=jnp.float32)
    grad_states = back(grad_embed)[0]
    return (grad_embed, grad_states)


def solution(mesh):
    in_specs = (
        P("dp", None, "mp"),
        P("mp"),
        P("mp", None),
        P("dp", None),
        P(("dp", "mp"), None, None),
        P(),
        P(),
        P(("dp", "mp"), None),
        P(("dp", "mp")),
    )
    out_specs = (P(("dp", "mp"), None), P(("dp", "mp"), None, None))
    return jax.shard_map(shards, mesh=mesh, in_specs=in_specs, out_specs=out_specs, check_vma=False)
```

profile of v0, /device:TPU:0, one launch (start us, length us, event | category | flops | bytes accessed | tf_op | source)
XLA Modules:
  0.0 156.2 jit_solution(10778247551571147130)
XLA Ops:
  7.2 0.0 all-reduce.2.cloned.1.call-start
  7.2 7.4 %fusion = f32[64,128]{1,0:T(8,128)S(1)} fusion(bf16[64,128,1024]{2,1,0:T(8,128)(2,1)} %param.9), kind=kLoop, calls=%fused_computation.2 | loop fusion | flops 25157632 | bytes 16809984 | tf_op jit(solution)/shard_map/reduce_sum | solution.py:41
  14.6 12.9 %psum.14 = f32[64,128]{1,0:T(8,128)S(1)} all-reduce(f32[64,128]{1,0:T(8,128)S(1)} %fusion), channel_id=1, replica_groups=mesh['dp'=8,'mp'=4] {'mp'}, use_global_device_ids=true, to_apply=%region_4.0 | all-reduce | flops 8192 | bytes 65536 | tf_op jit(solution)/shard_map/psum | solution.py:42
  27.6 7.6 %fusion.1 = f32[64,1024]{1,0:T(8,128)S(1)} fusion(bf16[64,128,1024]{2,1,0:T(8,128)(2,1)} %param.9, f32[64,128]{1,0:T(8,128)S(1)} %rsqrt_multiply_fusion), kind=kLoop, calls=%fused_computation.3 | loop fusion | flops 25100288 | bytes 17072128 | tf_op jit(solution)/shard_map/reduce_sum | solution.py:46
  35.3 1.2 fusion.31
  36.5 0.0 all-gather.2.cloned.1.call-start
  36.6 32.7 %all-reduce.2.cloned.1.call-done = f32[64,1024]{1,0:T(8,128)} async-done(((f32[64,1024]{1,0:T(8,128)}), f32[64,1024]{1,0:T(8,128)}) %all-reduce.2.cloned.1.call-update) | async-done | bytes 262160 | tf_op jit(solution)/shard_map/psum | solution.py:49
  69.2 1.1 multiply_reduce_fusion.1
  70.3 1.7 %multiply_convert_fusion = bf16[64,1024]{1,0:T(8,128)(2,1)} fusion(f32[64,1024]{1,0:T(8,128)} %all-reduce.2.cloned.1.call-done, f32[64]{0:T(128)S(1)} %add_rsqrt_fusion), kind=kLoop, calls=%fused_computation.43 | loop fusion | flops 196608 | bytes 393472 | tf_op jit(solution)/shard_map/convert_element_type | solution.py:50
  72.1 0.1 mul.250
  72.2 2.7 %fusion.17 = f32[32,64]{1,0:T(8,128)S(1)} fusion(bf16[32,64,768]{2,1,0:T(8,128)(2,1)} %param.13), kind=kLoop, calls=%fused_computation.28 | loop fusion | flops 4716544 | bytes 3153920 | tf_op jit(solution)/shard_map/jvp()/reduce_sum | solution.py:19
  74.9 2.7 %fusion.19 = bf16[32,64,768]{2,1,0:T(8,128)(2,1)S(1)} fusion(bf16[32,64,768]{2,1,0:T(8,128)(2,1)} %param.13, f32[768]{0:T(1024)S(1)} %copy-done.5, f32[32,64]{1,0:T(8,128)S(1)} %fusion.40), kind=kLoop, calls=%fused_computation.30 | loop fusion | flops 6291456 | bytes 6302720 | tf_op jit(solution)/shard_map/jvp()/convert_element_type | solution.py:20
  77.6 7.7 %multiply_reduce_fusion = (f32[32,1024]{1,0:T(8,128)S(1)}, f32[2048,1024]{1,0:T(8,128)}) fusion(f32[32,64]{1,0:T(8,128)S(1)} %convert_element_type.45, bf16[2048,768]{1,0:T(8,128)(2,1)S(1)} %bitcast.31, bf16[768,1024]{1,0:T(8,128)(2,1)S(1)} %copy-done.3), kind=kOutput, calls=%fused_computation.25 | convolution fusion | flops 3242164224 | bytes 13246464 | tf_op jit(solution)/shard_map/jvp()/dot_general | solution.py:22
  85.3 0.1 multiply_reduce_fusion.3
  85.4 27.1 %all-gather.2.cloned.1.call-done = bf16[512,1024]{1,0:T(8,128)(2,1)} async-done(((bf16[64,1024]{1,0:T(8,128)(2,1)}), bf16[512,1024]{1,0:T(8,128)(2,1)}) %all-gather.2.cloned.1.call-update) | async-done | bytes 1048592 | tf_op jit(solution)/shard_map/all_gather | solution.py:51
  112.5 2.5 %fusion.45 = (f32[32]{0:T(128)S(1)}, f32[32,512]{1,0:T(8,128)S(1)}) fusion(bf16[512,1024]{1,0:T(8,128)(2,1)} %all-gather.2.cloned.1.call-done, s32[32]{0:T(128)S(1)} %copy-done.9), kind=kOutput, calls=%fused_computation.73 | convolution fusion | flops 67190752 | bytes 1114368 | tf_op jit(solution)/shard_map/dot_general | solution.py:59
  115.0 1.8 %fusion.46 = (f32[32]{0:T(128)S(1)}, f32[32,512]{1,0:T(8,128)S(1)}) fusion(bf16[512,1024]{1,0:T(8,128)(2,1)} %all-gather.2.cloned.1.call-done, f32[32,1024]{1,0:T(8,128)S(1)} %get-tuple-element.8, f32[32]{0:T(128)S(1)} %fusion.41), kind=kOutput, calls=%fused_computation.74 | convolution fusion | flops 33685472 | bytes 1245440 | tf_op jit(solution)/shard_map/dot_general | solution.py:60
  116.7 1.7 %multiply_reduce_fusion.2 = (f32[32]{0:T(128)S(1)}, f32[32,1024]{1,0:T(8,128)S(1)}) fusion(f32[32,1024]{1,0:T(8,128)S(1)} %get-tuple-element.8, bf16[512,1024]{1,0:T(8,128)(2,1)} %all-gather.2.cloned.1.call-done, f32[32,512]{1,0:T(8,128)S(1)} %get-tuple-element.11, f32[32,512]{1,0:T(8,128)S(1)} %get-tuple-element.13, f32[32]{0:T(128)S(1)} %get-tuple-element.10, ...), kind=kOutput, calls=%fused_computation.48 | convolution fusion | flops 33718240 | bytes 1442176 | tf_op jit(solution)/shard_map/dot_general | solution.py:66
  118.4 0.7 add_add_fusion.1
  119.1 11.1 %fusion.14 = (f32[2048,1024]{1,0:T(8,128)}, f32[2048,1024]{1,0:T(8,128)}) fusion(f32[2048,1024]{1,0:T(8,128)} %get-tuple-element.9, f32[2048]{0:T(1024)S(1)} %mul.250, f32[32,1024]{1,0:T(8,128)S(1)} %get-tuple-element.4), kind=kLoop, calls=%fused_computation.23 | loop fusion | flops 33554432 | bytes 25305088 | tf_op jit(solution)/shard_map/transpose(jvp())/mul | solution.py:22
  130.2 11.6 %fusion.24 = bf16[2048,768]{1,0:T(8,128)(2,1)} fusion(bf16[768,1024]{1,0:T(8,128)(2,1)S(1)} %copy-done.4, f32[2048,1024]{1,0:T(8,128)} %get-tuple-element.3, f32[2048,1024]{1,0:T(8,128)S(1)} %bitcast.29, f32[2048,1024]{1,0:T(8,128)} %get-tuple-element.2), kind=kOutput, calls=%fused_computation.36 | convolution fusion | flops 3233284096 | bytes 29884416 | tf_op jit(solution)/shard_map/transpose(jvp())/dot_general | solution.py:22
  141.9 4.1 %fusion.20 = f32[32,64]{1,0:T(8,128)S(1)} fusion(bf16[32,64,768]{2,1,0:T(8,128)(2,1)} %param.13, bf16[32,64,768]{2,1,0:T(8,128)(2,1)} %bitcast.30, f32[768]{0:T(1024)S(1)} %copy-done.5), kind=kLoop, calls=%fused_computation.31 | loop fusion | flops 7862272 | bytes 6302720 | tf_op jit(solution)/shard_map/transpose(jvp())/reduce_sum | solution.py:20
  146.0 0.6 copy-done.2
  146.6 2.8 %fusion.16 = bf16[32,64,768]{2,1,0:T(8,128)(2,1)} fusion(bf16[32,64,768]{2,1,0:T(8,128)(2,1)S(1)} %copy-done.1, f32[32,64]{1,0:T(8,128)S(1)} %multiply_multiply_fusion.3, f32[768]{0:T(1024)S(1)} %copy-done.5, f32[32,64]{1,0:T(8,128)S(1)} %fusion.40, bf16[2048,768]{1,0:T(8,128)(2,1)S(1)} %copy-done.2), kind=kLoop, calls=%fused_computation.27 | loop fusion | flops 12582912 | bytes 9456640 | tf_op jit(solution)/shard_map/transpose(jvp())/convert_element_type | solution.py:18
  (33 shorter events, 0.2 us)
Async XLA Ops:
  7.2 28.1 %copy-start = (bf16[1024,1024]{1,0:T(8,128)(2,1)S(1)}, bf16[1024,1024]{1,0:T(8,128)(2,1)}, u32[]{:S(2)}) copy-start(bf16[1024,1024]{1,0:T(8,128)(2,1)} %param.11) | copy-start | bytes 6291460
  7.2 20.4 %copy-start.6 = (s32[64,128]{1,0:T(8,128)S(1)}, s32[64,128]{1,0:T(8,128)}, u32[]{:S(2)}) copy-start(s32[64,128]{1,0:T(8,128)} %param.12) | copy-start | bytes 98308
  7.2 62.1 %all-reduce.2.cloned.1.call-start = ((), (), s32[]{:S(2)}) async-start(), calls=%async_computation | async-start | bytes 524288 | tf_op jit(solution)/shard_map/psum | solution.py:49
  27.6 7.7 %copy-start.8 = (f32[1024]{0:T(1024)S(1)}, f32[1024]{0:T(1024)}, u32[]{:S(2)}) copy-start(f32[1024]{0:T(1024)} %param.10) | copy-start | bytes 12292
  27.6 44.5 %copy-start.7 = (s32[32,64]{1,0:T(8,128)S(1)}, s32[32,64]{1,0:T(8,128)}, u32[]{:S(2)}) copy-start(s32[32,64]{1,0:T(8,128)} %param.16) | copy-start | bytes 24580
  27.6 47.2 %copy-start.5 = (f32[768]{0:T(1024)S(1)}, f32[768]{0:T(1024)}, u32[]{:S(2)}) copy-start(f32[768]{0:T(1024)} %param.14) | copy-start | bytes 9220
  36.5 76.0 %all-gather.2.cloned.1.call-start = ((), (), s32[]{:S(2)}) async-start(), calls=%async_computation.1 | async-start | bytes 1179648 | tf_op jit(solution)/shard_map/all_gather | solution.py:51
  72.2 5.4 %copy-start.3 = (bf16[768,1024]{1,0:T(8,128)(2,1)S(1)}, bf16[768,1024]{1,0:T(8,128)(2,1)}, u32[]{:S(2)}) copy-start(bf16[768,1024]{1,0:T(8,128)(2,1)} %param.15) | copy-start | bytes 4718596
  74.9 37.6 %copy-start.9 = (s32[32]{0:T(128)S(1)}, s32[32]{0:T(128)}, u32[]{:S(2)}) copy-start(s32[32]{0:T(128)} %param.17) | copy-start | bytes 388
  118.4 11.8 %slice-start = ((s8[8388608]{0:T(1024)(128)(4,1)}), s8[4194304]{0:T(1024)(128)(4,1)S(1)}, s32[]{:S(2)}) async-start(s8[8388608]{0:T(1024)(128)(4,1)} %bitcast.28), calls=%async_computation.2 | async-start | bytes 8388608
  119.1 11.1 %slice-start.1 = ((s8[8388608]{0:T(1024)(128)(4,1)}), s8[4194304]{0:T(1024)(128)(4,1)S(1)}, s32[]{:S(2)}) async-start(s8[8388608]{0:T(1024)(128)(4,1)} %bitcast.28), calls=%async_computation.3 | async-start | bytes 8388608
  119.1 11.1 %copy-start.4 = (bf16[768,1024]{1,0:T(8,128)(2,1)S(1)}, bf16[768,1024]{1,0:T(8,128)(2,1)}, u32[]{:S(2)}) copy-start(bf16[768,1024]{1,0:T(8,128)(2,1)} %param.15) | copy-start | bytes 4718596
  141.9 4.1 %copy-start.1 = (bf16[32,64,768]{2,1,0:T(8,128)(2,1)S(1)}, bf16[32,64,768]{2,1,0:T(8,128)(2,1)}, u32[]{:S(2)}) copy-start(bf16[32,64,768]{2,1,0:T(8,128)(2,1)} %param.13) | copy-start | bytes 9437188
  141.9 4.7 %copy-start.2 = (bf16[2048,768]{1,0:T(8,128)(2,1)S(1)}, bf16[2048,768]{1,0:T(8,128)(2,1)}, u32[]{:S(2)}) copy-start(bf16[2048,768]{1,0:T(8,128)(2,1)} %fusion.24) | copy-start | bytes 9437188
Sparse Core Ops, SparseCore 0:
  36.6 32.5 all-reduce.1
  72.2 40.2 all-gather.1
where the time goes:
time: 157 us; the launch traced here: 156 us
  waiting for transfers between devices  59.8 us (38%)
  other arithmetic  41.9 us (27%)
  matrix products  26.5 us (17%)
  between operations  14.2 us (9%)
  blocking collectives  12.9 us (8%)
    psum x1, waiting for transfers between devices, shards(): summed = lax.psum(partial_embed, 'mp')  32.7 us
    all_gather x1, waiting for transfers between devices, shards(): gathered = lax.all_gather(group_emb, 'dp', axis=0, tiled=True)  27.1 us
    dot_general x2, matrix products, student_forward(): jnp.dot(flat, proj, preferred_element_type=jnp.float32)  19.3 us
    psum x1, blocking collectives, shards(): squares = lax.psum(partial_squares, 'mp')  12.9 us
    mul x1, other arithmetic, student_forward(): jax.nn.gelu(jnp.dot(flat, proj, preferred_element_type=jnp.float32), appr...  11.1 us
    reduce_sum x1, other arithmetic, shards(): pooled = jnp.sum(values * weight[:, :, None], axis=1)  7.65 us
    reduce_sum x1, other arithmetic, shards(): partial_squares = jnp.sum(values * values, axis=-1)  7.38 us
    reduce_sum x1, other arithmetic, student_forward(): normed = (values * scale * gain).astype(jnp.bfloat16)  4.07 us
  transfers between devices with their start and end apart: 2, of which 2 were waited for; matrix products, arithmetic and copies ran while one was open for 8% of the time, Pallas kernels for 0%

commit v1 on v0

--- a/solution.py
+++ b/solution.py
@@ -48,7 +48,12 @@
     partial_embed = jnp.dot(tpooled, teacher_proj, preferred_element_type=jnp.float32)
     summed = lax.psum(partial_embed, "mp")
     group_emb = unit_rows(summed).astype(jnp.bfloat16)
-    gathered = lax.all_gather(group_emb, "dp", axis=0, tiled=True)
+    ring = [group_emb]
+    for hop in range(7):
+        ring.append(lax.ppermute(ring[-1], "dp", [(dev, (dev + 1) % 8) for dev in range(8)]))
+    gathered = jnp.roll(
+        jnp.concatenate(ring[::-1], axis=0), (lax.axis_index("dp") + 1) * ring[0].shape[0], axis=0
+    )
     semb, back = jax.vjp(
         lambda st: student_forward(st, student_gain, student_proj, student_mask), student_states
     )

time: 157 us -> 188 us (1.20)
  waiting for transfers between devices: 59.8 us -> 76.3 us
  local copies, waits for them, and re-layouts: 0.73 us -> 10 us
  other arithmetic: 41.9 us -> 44.3 us
    ppermute x0 -> x7, waiting for transfers between devices: none -> 43.6 us  [shards(): lax.ppermute(ring[-1], 'dp', [(dev, (dev + 1) % 8) for dev in range(8)])]
    all_gather x1 -> x0, waiting for transfers between devices: 27.1 us -> none  [shards(): gathered = lax.all_gather(group_emb, 'dp', axis=0, tiled=True)]
    unnamed x24 -> x38, local copies, waits for them, and re-layouts: 0.66 us -> 9.95 us
  transfers between devices with their start and end apart: 2 -> 8, of which waited for: 2 -> 7; matrix products, arithmetic and copies ran while one was open for 8% -> 9% of each run, Pallas kernels for 0% -> 0%
where the time goes in v1:
time: 188 us
  waiting for transfers between devices  76.3 us (41%)
  other arithmetic  44.3 us (24%)
  matrix products  28 us (15%)
  between operations  14.2 us (8%)
  blocking collectives  12.9 us (7%)
  local copies, waits for them, and re-layouts  10 us (5%)
    ppermute x7, waiting for transfers between devices, shards(): lax.ppermute(ring[-1], 'dp', [(dev, (dev + 1) % 8) for dev in range(8)])  43.6 us
    psum x1, waiting for transfers between devices, shards(): summed = lax.psum(partial_embed, 'mp')  32.7 us
    dot_general x2, matrix products, student_forward(): jnp.dot(flat, proj, preferred_element_type=jnp.float32)  21 us
    psum x1, blocking collectives, shards(): squares = lax.psum(partial_squares, 'mp')  12.9 us
    mul x1, other arithmetic, student_forward(): jax.nn.gelu(jnp.dot(flat, proj, preferred_element_type=jnp.float32), appr...  11.1 us
    unnamed x38, local copies, waits for them, and re-layouts  9.95 us
    reduce_sum x1, other arithmetic, shards(): pooled = jnp.sum(values * weight[:, :, None], axis=1)  7.65 us
    reduce_sum x1, other arithmetic, shards(): partial_squares = jnp.sum(values * values, axis=-1)  7.38 us
  transfers between devices with their start and end apart: 8, of which 7 were waited for; matrix products, arithmetic and copies ran while one was open for 9% of the time, Pallas kernels for 0%

profile of v1, /device:TPU:0, one launch (start us, length us, event | category | flops | bytes accessed | tf_op | source)
XLA Modules:
  0.0 187.6 jit_solution(16814727736731190001)
XLA Ops:
  7.2 7.4 %fusion = f32[64,128]{1,0:T(8,128)S(1)} fusion(bf16[64,128,1024]{2,1,0:T(8,128)(2,1)} %param.9), kind=kLoop, calls=%fused_computation.2 | loop fusion | flops 25157632 | bytes 16809984 | tf_op jit(solution)/shard_map/reduce_sum | solution.py:41
  14.6 12.9 %psum.14 = f32[64,128]{1,0:T(8,128)S(1)} all-reduce(f32[64,128]{1,0:T(8,128)S(1)} %fusion), channel_id=1, replica_groups=mesh['dp'=8,'mp'=4] {'mp'}, use_global_device_ids=true, to_apply=%region_4.0 | all-reduce | flops 8192 | bytes 65536 | tf_op jit(solution)/shard_map/psum | solution.py:42
  27.6 7.6 %fusion.1 = f32[64,1024]{1,0:T(8,128)S(1)} fusion(bf16[64,128,1024]{2,1,0:T(8,128)(2,1)} %param.9, f32[64,128]{1,0:T(8,128)S(1)} %rsqrt_multiply_fusion), kind=kLoop, calls=%fused_computation.3 | loop fusion | flops 25100288 | bytes 17072128 | tf_op jit(solution)/shard_map/reduce_sum | solution.py:46
  35.3 1.2 fusion.36
  36.5 32.7 %all-reduce.2.cloned.1.call-done = f32[64,1024]{1,0:T(8,128)} async-done(((f32[64,1024]{1,0:T(8,128)}), f32[64,1024]{1,0:T(8,128)}) %all-reduce.2.cloned.1.call-update) | async-done | bytes 262160 | tf_op jit(solution)/shard_map/psum | solution.py:49
  69.2 1.1 multiply_reduce_fusion.1
  70.3 1.0 multiply_convert_fusion
  71.4 1.5 collective-permute-start
  72.9 6.2 %collective-permute-done = bf16[64,1024]{1,0:T(8,128)(2,1)S(1)} collective-permute-done((bf16[64,1024]{1,0:T(8,128)(2,1)S(1)}, bf16[64,1024]{1,0:T(8,128)(2,1)S(1)}, u32[]{:S(2)}, u32[]{:S(2)}) %collective-permute-start) | collective-permute-done | bytes 131104 | tf_op jit(solution)/shard_map/ppermute | solution.py:53
  79.1 7.7 %collective-permute-done.1 = bf16[64,1024]{1,0:T(8,128)(2,1)S(1)} collective-permute-done((bf16[64,1024]{1,0:T(8,128)(2,1)S(1)}, bf16[64,1024]{1,0:T(8,128)(2,1)S(1)}, u32[]{:S(2)}, u32[]{:S(2)}) %collective-permute-start.1) | collective-permute-done | bytes 131104 | tf_op jit(solution)/shard_map/ppermute | solution.py:53
  86.8 7.7 %collective-permute-done.2 = bf16[64,1024]{1,0:T(8,128)(2,1)S(1)} collective-permute-done((bf16[64,1024]{1,0:T(8,128)(2,1)S(1)}, bf16[64,1024]{1,0:T(8,128)(2,1)S(1)}, u32[]{:S(2)}, u32[]{:S(2)}) %collective-permute-start.2) | collective-permute-done | bytes 131104 | tf_op jit(solution)/shard_map/ppermute | solution.py:53
  94.4 2.6 %fusion.17 = f32[32,64]{1,0:T(8,128)S(1)} fusion(bf16[32,64,768]{2,1,0:T(8,128)(2,1)} %param.13), kind=kLoop, calls=%fused_computation.28 | loop fusion | flops 4716544 | bytes 3153920 | tf_op jit(solution)/shard_map/jvp()/reduce_sum | solution.py:19
  97.0 5.9 %collective-permute-done.3 = bf16[64,1024]{1,0:T(8,128)(2,1)S(1)} collective-permute-done((bf16[64,1024]{1,0:T(8,128)(2,1)S(1)}, bf16[64,1024]{1,0:T(8,128)(2,1)S(1)}, u32[]{:S(2)}, u32[]{:S(2)}) %collective-permute-start.3) | collective-permute-done | bytes 131104 | tf_op jit(solution)/shard_map/ppermute | solution.py:53
  103.0 8.5 %collective-permute-done.4 = bf16[64,1024]{1,0:T(8,128)(2,1)S(1)} collective-permute-done((bf16[64,1024]{1,0:T(8,128)(2,1)S(1)}, bf16[64,1024]{1,0:T(8,128)(2,1)S(1)}, u32[]{:S(2)}, u32[]{:S(2)}) %collective-permute-start.4) | collective-permute-done | bytes 131104 | tf_op jit(solution)/shard_map/ppermute | solution.py:53
  111.4 4.3 %fusion.19 = bf16[32,64,768]{2,1,0:T(8,128)(2,1)} fusion(bf16[32,64,768]{2,1,0:T(8,128)(2,1)} %param.13, f32[768]{0:T(1024)S(1)} %copy-done.5, f32[32,64]{1,0:T(8,128)S(1)} %fusion.44), kind=kLoop, calls=%fused_computation.30 | loop fusion | flops 6291456 | bytes 6302720 | tf_op jit(solution)/shard_map/jvp()/convert_element_type | solution.py:20
  115.8 9.4 %multiply_reduce_fusion = (f32[32,1024]{1,0:T(8,128)S(1)}, f32[2048,1024]{1,0:T(8,128)}) fusion(f32[32,64]{1,0:T(8,128)S(1)} %convert_element_type.45, bf16[2048,768]{1,0:T(8,128)(2,1)} %bitcast.27, bf16[768,1024]{1,0:T(8,128)(2,1)} %param.15), kind=kOutput, calls=%fused_computation.25 | convolution fusion | flops 3242164224 | bytes 13246464 | tf_op jit(solution)/shard_map/jvp()/dot_general | solution.py:22
  125.6 7.6 %collective-permute-done.6 = bf16[64,1024]{1,0:T(8,128)(2,1)S(1)} collective-permute-done((bf16[64,1024]{1,0:T(8,128)(2,1)S(1)}, bf16[64,1024]{1,0:T(8,128)(2,1)S(1)}, u32[]{:S(2)}, u32[]{:S(2)}) %collective-permute-start.6) | collective-permute-done | bytes 131104 | tf_op jit(solution)/shard_map/ppermute | solution.py:53
  144.1 2.3 %fusion.53 = (f32[32]{0:T(128)S(1)}, f32[32,512]{1,0:T(8,128)S(1)}) fusion(bf16[1024,1024]{1,0:T(8,128)(2,1)} %constant_dynamic-update-slice_fusion, s32[]{:T(128)S(6)} %select_n.14, s32[32]{0:T(128)S(1)} %copy-done.9), kind=kOutput, calls=%fused_computation.95 | convolution fusion | flops 67190752 | bytes 2163968 | tf_op jit(solution)/shard_map/dot_general | solution.py:64
  146.3 1.8 fusion.56
  148.1 1.7 multiply_reduce_fusion.2
  150.5 11.1 %fusion.14 = (f32[2048,1024]{1,0:T(8,128)}, f32[2048,1024]{1,0:T(8,128)}) fusion(f32[2048,1024]{1,0:T(8,128)} %get-tuple-element.9, f32[2048]{0:T(1024)S(1)} %mul.254, f32[32,1024]{1,0:T(8,128)S(1)} %get-tuple-element.4), kind=kLoop, calls=%fused_computation.23 | loop fusion | flops 33554432 | bytes 25305088 | tf_op jit(solution)/shard_map/transpose(jvp())/mul | solution.py:22
  161.6 11.6 %fusion.24 = bf16[2048,768]{1,0:T(8,128)(2,1)} fusion(bf16[768,1024]{1,0:T(8,128)(2,1)S(1)} %copy-done.3, f32[2048,1024]{1,0:T(8,128)} %get-tuple-element.3, f32[2048,1024]{1,0:T(8,128)S(1)} %bitcast.25, f32[2048,1024]{1,0:T(8,128)} %get-tuple-element.2), kind=kOutput, calls=%fused_computation.36 | convolution fusion | flops 3233284096 | bytes 29884416 | tf_op jit(solution)/shard_map/transpose(jvp())/dot_general | solution.py:22
  173.3 4.1 %fusion.20 = f32[32,64]{1,0:T(8,128)S(1)} fusion(bf16[32,64,768]{2,1,0:T(8,128)(2,1)} %param.13, bf16[32,64,768]{2,1,0:T(8,128)(2,1)} %bitcast.26, f32[768]{0:T(1024)S(1)} %copy-done.5), kind=kLoop, calls=%fused_computation.31 | loop fusion | flops 7862272 | bytes 6302720 | tf_op jit(solution)/shard_map/transpose(jvp())/reduce_sum | solution.py:20
  177.9 2.8 %fusion.16 = bf16[32,64,768]{2,1,0:T(8,128)(2,1)} fusion(bf16[32,64,768]{2,1,0:T(8,128)(2,1)S(1)} %copy-done.1, f32[32,64]{1,0:T(8,128)S(1)} %multiply_multiply_fusion.3, f32[768]{0:T(1024)S(1)} %copy-done.5, f32[32,64]{1,0:T(8,128)S(1)} %fusion.44, bf16[2048,768]{1,0:T(8,128)(2,1)S(1)} %copy-done.2), kind=kLoop, calls=%fused_computation.27 | loop fusion | flops 12582912 | bytes 9456640 | tf_op jit(solution)/shard_map/transpose(jvp())/convert_element_type | solution.py:18
  (60 shorter events, 12.7 us)
Async XLA Ops:
  7.2 28.1 %copy-start = (bf16[1024,1024]{1,0:T(8,128)(2,1)S(1)}, bf16[1024,1024]{1,0:T(8,128)(2,1)}, u32[]{:S(2)}) copy-start(bf16[1024,1024]{1,0:T(8,128)(2,1)} %param.11) | copy-start | bytes 6291460
  7.2 20.4 %copy-start.6 = (s32[64,128]{1,0:T(8,128)S(1)}, s32[64,128]{1,0:T(8,128)}, u32[]{:S(2)}) copy-start(s32[64,128]{1,0:T(8,128)} %param.12) | copy-start | bytes 98308
  7.2 62.1 %all-reduce.2.cloned.1.call-start = ((), (), s32[]{:S(2)}) async-start(), calls=%async_computation | async-start | bytes 524288 | tf_op jit(solution)/shard_map/psum | solution.py:49
  27.6 7.7 %copy-start.8 = (f32[1024]{0:T(1024)S(1)}, f32[1024]{0:T(1024)}, u32[]{:S(2)}) copy-start(f32[1024]{0:T(1024)} %param.10) | copy-start | bytes 12292
  35.3 76.2 %copy-start.5 = (f32[768]{0:T(1024)S(1)}, f32[768]{0:T(1024)}, u32[]{:S(2)}) copy-start(f32[768]{0:T(1024)} %param.14) | copy-start | bytes 9220
  35.3 80.5 %copy-start.7 = (s32[32,64]{1,0:T(8,128)S(1)}, s32[32,64]{1,0:T(8,128)}, u32[]{:S(2)}) copy-start(s32[32,64]{1,0:T(8,128)} %param.16) | copy-start | bytes 24580
  71.4 7.7 %collective-permute-start = (bf16[64,1024]{1,0:T(8,128)(2,1)S(1)}, bf16[64,1024]{1,0:T(8,128)(2,1)S(1)}, u32[]{:S(2)}, u32[]{:S(2)}) collective-permute-start(bf16[64,1024]{1,0:T(8,128)(2,1)S(1)} %multiply_convert_fusion), channel_id=1, source_target_pairs={{0,4},{4,8},{8,12},{12,16},{16,20},{20,24},{24,28},{28,0},{1,5},{5... | collective-permute-start | bytes 393224 | tf_op jit(solution)/shard_map/ppermute | solution.py:53
  79.1 7.7 %collective-permute-start.1 = (bf16[64,1024]{1,0:T(8,128)(2,1)S(1)}, bf16[64,1024]{1,0:T(8,128)(2,1)S(1)}, u32[]{:S(2)}, u32[]{:S(2)}) collective-permute-start(bf16[64,1024]{1,0:T(8,128)(2,1)S(1)} %collective-permute-done), channel_id=1, source_target_pairs={{0,4},{4,8},{8,12},{12,16},{16,20},{20,24},{24,28},{28,0},{1,5},{5... | collective-permute-start | bytes 393224 | tf_op jit(solution)/shard_map/ppermute | solution.py:53
  86.8 7.7 %collective-permute-start.2 = (bf16[64,1024]{1,0:T(8,128)(2,1)S(1)}, bf16[64,1024]{1,0:T(8,128)(2,1)S(1)}, u32[]{:S(2)}, u32[]{:S(2)}) collective-permute-start(bf16[64,1024]{1,0:T(8,128)(2,1)S(1)} %collective-permute-done.1), channel_id=1, source_target_pairs={{0,4},{4,8},{8,12},{12,16},{16,20},{20,24},{24,28},{28,0},{1,5},{5... | collective-permute-start | bytes 393224 | tf_op jit(solution)/shard_map/ppermute | solution.py:53
  94.4 8.5 %collective-permute-start.3 = (bf16[64,1024]{1,0:T(8,128)(2,1)S(1)}, bf16[64,1024]{1,0:T(8,128)(2,1)S(1)}, u32[]{:S(2)}, u32[]{:S(2)}) collective-permute-start(bf16[64,1024]{1,0:T(8,128)(2,1)S(1)} %collective-permute-done.2), channel_id=1, source_target_pairs={{0,4},{4,8},{8,12},{12,16},{16,20},{20,24},{24,28},{28,0},{1,5},{5... | collective-permute-start | bytes 393224 | tf_op jit(solution)/shard_map/ppermute | solution.py:53
  102.9 8.5 %collective-permute-start.4 = (bf16[64,1024]{1,0:T(8,128)(2,1)S(1)}, bf16[64,1024]{1,0:T(8,128)(2,1)S(1)}, u32[]{:S(2)}, u32[]{:S(2)}) collective-permute-start(bf16[64,1024]{1,0:T(8,128)(2,1)S(1)} %collective-permute-done.3), channel_id=1, source_target_pairs={{0,4},{4,8},{8,12},{12,16},{16,20},{20,24},{24,28},{28,0},{1,5},{5... | collective-permute-start | bytes 393224 | tf_op jit(solution)/shard_map/ppermute | solution.py:53
  111.4 13.9 %collective-permute-start.5 = (bf16[64,1024]{1,0:T(8,128)(2,1)S(1)}, bf16[64,1024]{1,0:T(8,128)(2,1)S(1)}, u32[]{:S(2)}, u32[]{:S(2)}) collective-permute-start(bf16[64,1024]{1,0:T(8,128)(2,1)S(1)} %collective-permute-done.4), channel_id=1, source_target_pairs={{0,4},{4,8},{8,12},{12,16},{16,20},{20,24},{24,28},{28,0},{1,5},{5... | collective-permute-start | bytes 393224 | tf_op jit(solution)/shard_map/ppermute | solution.py:53
  115.8 22.1 %copy-start.4 = (f32[64,1024]{1,0:T(8,128)S(1)}, f32[64,1024]{1,0:T(8,128)}, u32[]{:S(2)}) copy-start(f32[64,1024]{1,0:T(8,128)} %all-reduce.2.cloned.1.call-done) | copy-start | bytes 786436
  115.8 28.2 %copy-start.9 = (s32[32]{0:T(128)S(1)}, s32[32]{0:T(128)}, u32[]{:S(2)}) copy-start(s32[32]{0:T(128)} %param.17) | copy-start | bytes 388
  125.4 7.9 %collective-permute-start.6 = (bf16[64,1024]{1,0:T(8,128)(2,1)S(1)}, bf16[64,1024]{1,0:T(8,128)(2,1)S(1)}, u32[]{:S(2)}, u32[]{:S(2)}) collective-permute-start(bf16[64,1024]{1,0:T(8,128)(2,1)S(1)} %collective-permute-done.5), channel_id=1, source_target_pairs={{0,4},{4,8},{8,12},{12,16},{16,20},{20,24},{24,28},{28,0},{1,5},{5... | collective-permute-start | bytes 393224 | tf_op jit(solution)/shard_map/ppermute | solution.py:53
  149.8 11.8 %slice-start = ((s8[8388608]{0:T(1024)(128)(4,1)}), s8[4194304]{0:T(1024)(128)(4,1)S(1)}, s32[]{:S(2)}) async-start(s8[8388608]{0:T(1024)(128)(4,1)} %bitcast.24), calls=%async_computation.1 | async-start | bytes 8388608
  150.5 11.1 %slice-start.1 = ((s8[8388608]{0:T(1024)(128)(4,1)}), s8[4194304]{0:T(1024)(128)(4,1)S(1)}, s32[]{:S(2)}) async-start(s8[8388608]{0:T(1024)(128)(4,1)} %bitcast.24), calls=%async_computation.2 | async-start | bytes 8388608
  150.5 11.1 %copy-start.3 = (bf16[768,1024]{1,0:T(8,128)(2,1)S(1)}, bf16[768,1024]{1,0:T(8,128)(2,1)}, u32[]{:S(2)}) copy-start(bf16[768,1024]{1,0:T(8,128)(2,1)} %param.15) | copy-start | bytes 4718596
  173.2 4.1 %copy-start.1 = (bf16[32,64,768]{2,1,0:T(8,128)(2,1)S(1)}, bf16[32,64,768]{2,1,0:T(8,128)(2,1)}, u32[]{:S(2)}) copy-start(bf16[32,64,768]{2,1,0:T(8,128)(2,1)} %param.13) | copy-start | bytes 9437188
  173.2 4.7 %copy-start.2 = (bf16[2048,768]{1,0:T(8,128)(2,1)S(1)}, bf16[2048,768]{1,0:T(8,128)(2,1)}, u32[]{:S(2)}) copy-start(bf16[2048,768]{1,0:T(8,128)(2,1)} %fusion.24) | copy-start | bytes 9437188
Sparse Core Ops, SparseCore 0:
  36.6 32.5 all-reduce.1
